TPU v7x, 128 devices: a whole 4x4x4 slice. The times are simulated.
128 devices in a mesh: mode: 32 (over y_lo, z, x), var: 4 (over y_hi, core).
Axes of the slice: x: 4, y: 4 (y_hi: 2, y_lo: 2; y = y_hi * 2 + y_lo), z: 4, core: 2. Of those that a mesh axis runs over, the one named last changes fastest.
Arguments:
- control: bfloat16 [1, 4, 32, 1024, 1024], P(None, 'var', 'mode'), may hold values from -6 to 6
- filters: bfloat16 [3, 1024, 1024], replicated, may hold values from -4 to 5
- weights: bfloat16 [4, 3, 1024, 1024], P('var'), may hold values from 0.29882812 to 3
- vertical: bfloat16 [4, 64, 32], replicated, may hold values from -1 to 1
- balance: bfloat16 [3, 64, 64], replicated, may hold values from -0.75 to 0.75
Outputs:
- increment: bfloat16 [1, 4, 64, 1024, 1024], P(None, 'var', 'mode')
All inputs are finite; a program needn't handle non-finite values.
Results may differ from a plain program's by a relative error of at most 0.006.
Values may be sent and summed in bfloat16 or wider, within the bound.
No kernel may reach another device: no remote copies, remote signals or barrier semaphores. Data moves between devices by JAX's collectives and lax.ppermute only.
A program may use at most 64 MiB of HBM per device.

v0:
```python
import jax
import jax.numpy as jnp
from jax import lax
from jax.sharding import PartitionSpec as P


def in_blocks(shard, dim, size):
    lengths = shard.shape
    tiles = shard.reshape(*lengths[:dim], size, lengths[dim] // size, *lengths[dim + 1 :])
    return jnp.moveaxis(tiles, dim, 0)


def in_order(tiles, dim):
    tiles = jnp.moveaxis(tiles, 0, dim)
    lengths = tiles.shape
    return tiles.reshape(*lengths[:dim], lengths[dim] * lengths[dim + 1], *lengths[dim + 2 :])


def joined_exchange(shard, axis, axes, splits, concats):
    sizes = [lax.axis_size(a) for a in axes]
    tiles = in_blocks(shard, splits[0], sizes[0])
    tiles = jnp.moveaxis(in_blocks(tiles, splits[1] + 1, sizes[1]), 0, 1)
    inside = tiles.shape[2:]
    tiles = tiles.reshape(-1, *inside)
    tiles = lax.all_to_all(tiles, axis, split_axis=0, concat_axis=0, tiled=True)
    tiles = in_order(tiles.reshape(*sizes, *inside), concats[0] + 1)
    return in_order(tiles, concats[1])


def smooth(planes, filters, weights):
    total = jnp.zeros(planes.shape, jnp.float32)
    for k in range(filters.shape[0]):
        half = jnp.einsum(
            "ij,pjc->pic", filters[k], planes, preferred_element_type=jnp.float32
        ).astype(jnp.bfloat16)
        full = jnp.einsum("pic,dc->pid", half, filters[k], preferred_element_type=jnp.float32)
        total = total + weights[k].astype(jnp.float32) * full
    return total.astype(jnp.bfloat16)


def per_device(control, filters, weights, vertical, balance):
    members, _, depth, rows, cols = control.shape
    nmode = lax.axis_size("mode")
    nvar = lax.axis_size("var")
    strip = rows // (nmode * nvar)
    levcount = vertical.shape[1]
    filtered = smooth(control.reshape(members * depth, rows, cols), filters, weights[0])
    filtered = filtered.reshape(members, 1, depth, nvar, nmode, strip, cols)
    blocks = joined_exchange(filtered, ("mode", "var"), ("mode", "var"), (4, 3), (2, 1))
    modecount = blocks.shape[2]
    blocks = blocks.reshape(members, nvar, modecount, strip * cols)
    levels = jnp.einsum("vlq,mvqc->mvlc", vertical, blocks, preferred_element_type=jnp.float32)
    stream = levels[:, 0].astype(jnp.bfloat16)
    extra = jnp.einsum("vlk,mkc->mvlc", balance, stream, preferred_element_type=jnp.float32)
    result = jnp.concatenate([levels[:, :1], levels[:, 1:] + extra], axis=1).astype(jnp.bfloat16)
    result = result.reshape(members, nvar, levcount, 1, 1, strip, cols)
    back = joined_exchange(result, ("mode", "var"), ("mode", "var"), (2, 1), (4, 3))
    return back.reshape(members, 1, levcount // nmode, rows, cols)


def solution(mesh):
    in_specs = (P(None, "var", "mode", None, None), P(), P("var", None, None, None), P(), P())
    out_specs = P(None, "var", "mode", None, None)
    return jax.shard_map(
        per_device, mesh=mesh, in_specs=in_specs, out_specs=out_specs, check_vma=False
    )
```

profile of v0, /device:TPU:1, one launch (start us, length us, event | category | flops | bytes accessed | tf_op | source)
XLA Modules:
  0.0 148.6 jit_solution(3320128012047261081)
XLA Ops:
  0.0 0.0 copy-start
  0.0 1.6 %copy-done = bf16[1,1,1,1024,1024]{4,3,2,1,0:T(8,128)(2,1)S(1)} copy-done((bf16[1,1,1,1024,1024]{4,3,2,1,0:T(8,128)(2,1)S(1)}, bf16[1,1,1,1024,1024]{4,3,2,1,0:T(8,128)(2,1)}, u32[]{:S(2)}) %copy-start) | copy-done | bytes 2097176
  1.6 8.8 %fusion.6 = f32[1024,1024]{1,0:T(8,128)} fusion(bf16[3,1024,1024]{2,1,0:T(8,128)(2,1)} %param.6, bf16[1,1,1,1024,1024]{4,3,2,1,0:T(8,128)(2,1)S(1)} %copy-done), kind=kOutput, calls=%fused_computation.13 | convolution fusion | flops 4296015872 | bytes 10485760 | tf_op jit(solution)/shard_map/pic,dc->pid/dot_general | solution.py:36
  10.4 8.8 %fusion.8 = f32[1024,1024]{1,0:T(8,128)} fusion(bf16[3,1024,1024]{2,1,0:T(8,128)(2,1)} %param.6, bf16[1,1,1,1024,1024]{4,3,2,1,0:T(8,128)(2,1)S(1)} %copy-done), kind=kOutput, calls=%fused_computation.15 | convolution fusion | flops 4296015872 | bytes 10485760 | tf_op jit(solution)/shard_map/pic,dc->pid/dot_general | solution.py:36
  19.1 12.8 %fusion.3 = bf16[1024,1024]{1,0:T(8,128)(2,1)} fusion(f32[1024,1024]{1,0:T(8,128)} %fusion.6, f32[1024,1024]{1,0:T(8,128)} %fusion.8, bf16[1,3,1024,1024]{3,2,1,0:T(8,128)(2,1)} %param.7, bf16[3,1024,1024]{2,1,0:T(8,128)(2,1)} %param.6, bf16[1,1,1,1024,1024]{4,3,2,1,0:T(8,128)(2,1)S(1)} %copy-done), kind=kOutput, calls=%fused_computation.7 | convolution fusion | flops 4305453056 | bytes 23068672 | tf_op jit(solution)/shard_map/pic,dc->pid/dot_general | solution.py:36
  32.0 1.8 %copy.16 = bf16[1,1,1,4,32,1,8,1024]{7,6,3,4,5,2,1,0:T(8,128)(2,1)S(1)} copy(bf16[1,1,1,4,32,1,8,1024]{7,6,4,3,5,2,1,0:T(8,128)(2,1)} %bitcast.143) | data formatting | bytes 4194304 | tf_op jit(solution)/shard_map/reshape;reshape | solution.py:9
  33.7 41.6 %all_to_all.10 = bf16[128,1,1,1,1,1,8,1024]{7,6,5,4,3,2,1,0:T(8,128)(2,1)} all-to-all(bf16[128,1,1,1,1,1,8,1024]{7,6,5,4,3,2,1,0:T(8,128)(2,1)S(1)} %bitcast.139), channel_id=1, replica_groups=mesh['mode'=32,'var'=4] {'mode','var'}, dimensions={0} | all-to-all | bytes 4194304 | tf_op jit(solution)/shard_map/all_to_all | solution.py:25
  75.3 0.0 copy-start.2
  75.3 4.5 %reshape.119 = bf16[4,32,8192]{2,0,1:T(4,128)(2,1)} reshape(bf16[4,1,1,32,1,1,1,8,1024]{8,7,0,3,6,5,4,2,1:T(8,128)(2,1)} %bitcast.140) | data formatting | bytes 4194304 | tf_op jit(solution)/shard_map/reshape.22
  79.8 0.0 copy-done.2
  79.8 0.0 copy-start.1
  79.8 4.8 %convolution_bitcast_fusion = f32[1,4,64,8192]{3,2,1,0:T(8,128)S(1)} fusion(bf16[4,64,32]{1,2,0:T(8,128)(2,1)S(1)} %copy-done.2, bf16[4,32,8192]{2,0,1:T(4,128)(2,1)} %reshape.119), kind=kOutput, calls=%fused_computation | convolution fusion | flops 134217728 | bytes 10502144 | tf_op jit(solution)/shard_map/vlq,mvqc->mvlc/dot_general | solution.py:52
  84.7 0.1 slice.82
  84.8 0.0 copy-done.1
  84.8 1.0 fusion.1
  85.8 2.2 %copy.25 = bf16[24,8,8,1024]{3,2,1,0:T(8,128)(2,1)S(1)} copy(bf16[24,8,8,1024]{3,1,2,0:T(8,128)(2,1)S(1)} %bitcast.135) | data formatting | bytes 6291456
  87.9 0.6 copy.24
  88.5 0.6 pad_maximum_fusion
  89.2 56.7 %all_to_all.11 = bf16[128,1,1,2,1,1,8,1024]{7,6,3,5,4,2,1,0:T(8,128)(2,1)S(1)} all-to-all(bf16[128,1,1,2,1,1,8,1024]{7,6,3,5,4,2,1,0:T(8,128)(2,1)S(1)} %bitcast.136), channel_id=1, replica_groups=mesh['mode'=32,'var'=4] {'mode','var'}, dimensions={0} | all-to-all | bytes 8388608 | tf_op jit(solution)/shard_map/all_to_all | solution.py:25
  145.9 2.6 %copy.22 = bf16[1,1,2,4,1,32,8,1024]{7,6,5,3,2,4,1,0:T(8,128)(2,1)} copy(bf16[1,1,2,4,1,32,8,1024]{7,6,2,3,5,4,1,0:T(8,128)(2,1)S(1)} %bitcast.137) | data formatting | bytes 8388608 | tf_op jit(solution)/shard_map/transpose | solution.py:14
Async XLA Ops:
  0.0 1.6 %copy-start = (bf16[1,1,1,1024,1024]{4,3,2,1,0:T(8,128)(2,1)S(1)}, bf16[1,1,1,1024,1024]{4,3,2,1,0:T(8,128)(2,1)}, u32[]{:S(2)}) copy-start(bf16[1,1,1,1024,1024]{4,3,2,1,0:T(8,128)(2,1)} %param.5) | copy-start | bytes 6291460
  75.3 4.5 %copy-start.2 = (bf16[4,64,32]{1,2,0:T(8,128)(2,1)S(1)}, bf16[4,64,32]{1,2,0:T(8,128)(2,1)}, u32[]{:S(2)}) copy-start(bf16[4,64,32]{1,2,0:T(8,128)(2,1)} %param.8) | copy-start | bytes 49156
  79.8 5.0 %copy-start.1 = (bf16[3,64,64]{2,1,0:T(8,128)(2,1)S(1)}, bf16[3,64,64]{2,1,0:T(8,128)(2,1)}, u32[]{:S(2)}) copy-start(bf16[3,64,64]{2,1,0:T(8,128)(2,1)} %param.9) | copy-start | bytes 73732
where the time goes:
time: 150 us; the launch traced here: 149 us
  blocking collectives  98.3 us (66%)
  matrix products  36.2 us (24%)
  local copies, waits for them, and re-layouts  13.4 us (9%)
    all_to_all x2, blocking collectives, joined_exchange(): tiles = lax.all_to_all(tiles, axis, split_axis=0, concat_axis=0, tiled=True)  98.3 us
    dot_general x3, matrix products, smooth(): jnp.einsum('pic,dc->pid', half, filters[k], preferred_element_type=jnp.fl...  30.4 us
    dot_general x1, matrix products, per_device(): jnp.einsum('vlq,mvqc->mvlc', vertical, blocks, preferred_element_type=jnp...  4.84 us
    another operation x1, local copies, waits for them, and re-layouts  4.49 us
    unnamed x8, local copies, waits for them, and re-layouts  4.37 us

commit v1 on v0

v1 whole, which is shorter than its diff:
```python
import jax
import jax.numpy as jnp
from jax import lax
from jax.experimental import pallas as pl
from jax.experimental.pallas import tpu as pltpu
from jax.sharding import PartitionSpec as P

SUB = 8
WIDE = 256
MB = 2**20


def vmem(mib):
    return pltpu.CompilerParams(vmem_limit_bytes=mib * MB)


def cost(flops, nbytes):
    return pl.CostEstimate(flops=int(flops), bytes_accessed=int(nbytes), transcendentals=0)


def spread(small, contract):
    cols = small.shape[contract]
    rows = small.shape[1 - contract]
    wide = cols * SUB
    lane = lax.broadcasted_iota(jnp.int32, (cols, wide), 1)
    source = lax.broadcasted_iota(jnp.int32, (cols, wide), 0)
    repeat = jnp.where(lane // SUB == source, 1.0, 0.0).astype(jnp.bfloat16)
    each = lax.dot_general(
        small, repeat, (((contract,), (0,)), ((), ())), preferred_element_type=jnp.float32
    )
    sub = lax.broadcasted_iota(jnp.int32, (rows, SUB, wide), 1)
    at = lax.broadcasted_iota(jnp.int32, (rows, SUB, wide), 2)
    tall = jnp.broadcast_to(each[:, None, :], (rows, SUB, wide))
    return jnp.where(at % SUB == sub, tall, 0.0).reshape(rows * SUB, wide).astype(jnp.bfloat16)


def smooth_kernel(
    plane_any, filters_any, weights_any, vertical_any, balance_any,
    out_ref, coeff_ref,
    plane_ref, filters_ref, weights_ref, vertical_ref, balance_ref, half_ref, total_ref, sems,
):
    count = filters_ref.shape[0]
    small = [
        pltpu.make_async_copy(vertical_any, vertical_ref, sems.at[2 * count + 1]),
        pltpu.make_async_copy(balance_any, balance_ref, sems.at[2 * count + 2]),
    ]
    plane = pltpu.make_async_copy(plane_any, plane_ref, sems.at[2 * count])
    filters = [
        pltpu.make_async_copy(filters_any.at[k], filters_ref.at[k], sems.at[2 * k])
        for k in range(count)
    ]
    weights = [
        pltpu.make_async_copy(weights_any.at[k], weights_ref.at[k], sems.at[2 * k + 1])
        for k in range(count)
    ]
    for copy in small:
        copy.start()
    plane.start()
    for k in range(count):
        filters[k].start()
        weights[k].start()

    for copy in small:
        copy.wait()
    modes = vertical_ref.shape[1] * SUB
    for v in range(vertical_ref.shape[0]):
        coeff_ref[v, :, :modes] = spread(vertical_ref[v], 0)
        if v:
            coeff_ref[v, :, modes:] = spread(balance_ref[v - 1], 1)

    plane.wait()
    for k in range(count):
        filters[k].wait()
        half_ref[...] = jnp.dot(
            filters_ref[k], plane_ref[...], preferred_element_type=jnp.float32
        ).astype(jnp.bfloat16)
        weights[k].wait()
        full = lax.dot_general(
            half_ref[...], filters_ref[k], (((1,), (1,)), ((), ())),
            preferred_element_type=jnp.float32,
        )
        term = weights_ref[k].astype(jnp.float32) * full
        if k == 0:
            total_ref[...] = term
        elif k < count - 1:
            total_ref[...] += term
        else:
            out_ref[...] = (total_ref[...] + term).astype(jnp.bfloat16)


def smooth(plane, filters, weights, vertical, balance):
    count, size, _ = filters.shape
    nvar, modes, levs = vertical.shape
    return pl.pallas_call(
        smooth_kernel,
        out_shape=[
            jax.ShapeDtypeStruct((size, size), jnp.bfloat16),
            jax.ShapeDtypeStruct((nvar, levs * SUB, (modes + levs) * SUB), jnp.bfloat16),
        ],
        in_specs=[pl.BlockSpec(memory_space=pl.ANY)] * 5,
        scratch_shapes=[
            pltpu.VMEM(plane.shape, jnp.bfloat16),
            pltpu.VMEM(filters.shape, jnp.bfloat16),
            pltpu.VMEM(weights.shape, jnp.bfloat16),
            pltpu.VMEM(vertical.shape, jnp.bfloat16),
            pltpu.VMEM(balance.shape, jnp.bfloat16),
            pltpu.VMEM((size, size), jnp.bfloat16),
            pltpu.VMEM((size, size), jnp.float32),
            pltpu.SemaphoreType.DMA((2 * count + 3,)),
        ],
        cost_estimate=cost(4 * count * size**3, 18 * MB),
        compiler_params=pltpu.CompilerParams(vmem_limit_bytes=67043328),
        name="smooth",
    )(plane, filters, weights, vertical, balance)


def level_kernel(blocks_ref, coeff_ref, out_ref):
    nvar, modes, _, size = blocks_ref.shape
    deep = modes * SUB
    for first in range(0, size, WIDE):
        lanes = slice(first, first + WIDE)
        stream = None
        for v in range(nvar):
            block = blocks_ref[v, :, :, lanes].reshape(deep, WIDE)
            if v == 0:
                level = jnp.dot(coeff_ref[v, :, :deep], block, preferred_element_type=jnp.float32)
                level = stream = level.astype(jnp.bfloat16)
            else:
                level = jnp.dot(
                    coeff_ref[v],
                    jnp.concatenate([block, stream], axis=0),
                    preferred_element_type=jnp.float32,
                ).astype(jnp.bfloat16)
            shape = (out_ref.shape[1], out_ref.shape[2], SUB, WIDE)
            out_ref[v, :, :, :, lanes] = level.reshape(shape)


def mix_levels(blocks, coeff, nmode):
    nvar, modes, _, size = blocks.shape
    tall = coeff.shape[1]
    each = tall // SUB // nmode
    return pl.pallas_call(
        level_kernel,
        out_shape=jax.ShapeDtypeStruct((nvar, nmode, each, SUB, size), jnp.bfloat16),
        cost_estimate=cost(
            2 * tall * size * (nvar * modes * SUB + (nvar - 1) * tall), 8 * MB
        ),
        compiler_params=vmem(32),
        name="levels",
    )(blocks, coeff)


def place_kernel(back_ref, out_any, sems):
    tiles, levs = back_ref.shape[:2]
    some = tiles // sems.shape[1]
    copies = []
    for at in range(levs):
        for i in range(sems.shape[1]):
            rows = pl.ds(i * some, some)
            copies.append(
                pltpu.make_async_copy(back_ref.at[rows, at], out_any.at[at, rows], sems.at[at, i])
            )
    for copy in copies:
        copy.start()
    for copy in copies:
        copy.wait()


def place(back):
    tiles, levs, sub, size = back.shape
    return pl.pallas_call(
        place_kernel,
        out_shape=jax.ShapeDtypeStruct((levs, tiles, sub, size), jnp.bfloat16),
        in_specs=[pl.BlockSpec(memory_space=pltpu.VMEM)],
        out_specs=pl.BlockSpec(memory_space=pl.ANY),
        scratch_shapes=[pltpu.SemaphoreType.DMA((levs, 8))],
        cost_estimate=cost(2**29, 8 * MB),
        compiler_params=vmem(16),
        name="place",
    )(back)


def per_device(control, filters, weights, vertical, balance):
    size = control.shape[-1]
    nmode, nvar = lax.axis_size("mode"), lax.axis_size("var")
    count = nmode * nvar
    each = vertical.shape[1] // nmode
    axes = ("var", "mode")
    filtered, coeff = smooth(
        control[0, 0, 0], filters, weights[0], jnp.swapaxes(vertical, 1, 2), balance
    )
    blocks = lax.all_to_all(filtered.reshape(count, SUB, size), axes, 0, 0, tiled=True)
    result = mix_levels(blocks.reshape(nvar, nmode, SUB, size), coeff, nmode)
    back = lax.all_to_all(result.reshape(count, each, SUB, size), axes, 0, 0, tiled=True)
    return place(back).reshape(1, 1, each, size, size)


def solution(mesh):
    in_specs = (P(None, "var", "mode", None, None), P(), P("var", None, None, None), P(), P())
    out_specs = P(None, "var", "mode", None, None)
    return jax.shard_map(
        per_device, mesh=mesh, in_specs=in_specs, out_specs=out_specs, check_vma=False
    )
```

time: 150 us -> 120 us (0.80)
  matrix products: 36.2 us -> 0 us
  Pallas kernels: 0 us -> 22.9 us
  local copies, waits for them, and re-layouts: 13.4 us -> 0.01 us
  blocking collectives: 98.3 us -> 96.7 us
    dot_general x5 -> x0, matrix products: 36.2 us -> none  [the longest x3 30.4 us: smooth(): jnp.einsum('pic,dc->pid', half, filters[k], preferred_element_type=jnp.fl...]
    pallas_call x0 -> x3, Pallas kernels: none -> 22.9 us  [the longest x1 17.8 us: smooth(): pl.pallas_call(smooth_kernel, out_shape=[jax.ShapeDtypeStruct((size, size...]
    another operation x2 -> x0, local copies, waits for them, and re-layouts: 6.25 us -> none
    unnamed x8 -> x2, local copies, waits for them, and re-layouts: 4.37 us -> 0.01 us
    transpose x1 -> x0, local copies, waits for them, and re-layouts: 2.64 us -> none  [in_order(): tiles = jnp.moveaxis(tiles, 0, dim)]
    all_to_all x2, blocking collectives: 98.3 us -> 96.7 us  [the longest x1 56 us: per_device(): lax.all_to_all(result.reshape(count, each, SUB, size), axes, 0, 0, tiled=...]
where the time goes in v1:
time: 120 us
  blocking collectives  96.7 us (81%)
  Pallas kernels  22.9 us (19%)
    all_to_all x1, blocking collectives, per_device(): lax.all_to_all(result.reshape(count, each, SUB, size), axes, 0, 0, tiled=...  56 us
    all_to_all x1, blocking collectives, per_device(): lax.all_to_all(filtered.reshape(count, SUB, size), axes, 0, 0, tiled=True)  40.7 us
    pallas_call x1, Pallas kernels, smooth(): pl.pallas_call(smooth_kernel, out_shape=[jax.ShapeDtypeStruct((size, size...  17.8 us
    pallas_call x1, Pallas kernels, mix_levels(): pl.pallas_call(level_kernel, out_shape=jax.ShapeDtypeStruct((nvar, nmode,...  2.93 us

profile of v1, /device:TPU:1, one launch (start us, length us, event | category | flops | bytes accessed | tf_op | source)
XLA Modules:
  0.0 119.7 jit_solution(13126980706440715403)
XLA Ops:
  0.0 17.8 %smooth.1 = (bf16[1024,1024]{1,0:T(8,128)(2,1)}, bf16[4,512,768]{2,1,0:T(8,128)(2,1)}) custom-call(bf16[1024,1024]{1,0:T(8,128)(2,1)} %bitcast.11, bf16[3,1024,1024]{2,1,0:T(8,128)(2,1)} %filters_any.1, bf16[3,1024,1024]{2,1,0:T(8,128)(2,1)} %bitcast.10, bf16[4,32,64]{2,1,0:T(8,128)(2,1)} %bitcast.12, bf16[3,64,64]{2,1,0:T(8,128)(2,1)} %balance_any.1), custom_call_target="tpu_custom_call" | custom-call | flops 12884901888 | bytes 18874368 | tf_op jit(solution)/shard_map/smooth/pallas_call | solution.py:94
  17.8 0.0 copy-start
  17.8 40.7 %all_to_all.10 = bf16[128,8,1024]{2,1,0:T(8,128)(2,1)S(1)} all-to-all(bf16[128,8,1024]{2,1,0:T(8,128)(2,1)} %bitcast.9), channel_id=1, replica_groups=mesh['mode'=32,'var'=4] {'var','mode'}, dimensions={0} | all-to-all | bytes 4194304 | tf_op jit(solution)/shard_map/all_to_all | solution.py:192
  58.5 0.0 copy-done
  58.5 2.9 %levels.1 = bf16[4,32,2,8,1024]{4,3,2,1,0:T(8,128)(2,1)S(1)} custom-call(bf16[4,32,8,1024]{3,2,1,0:T(8,128)(2,1)S(1)} %bitcast.8, bf16[4,512,768]{2,1,0:T(8,128)(2,1)S(1)} %copy-done), custom_call_target="tpu_custom_call" | custom-call | flops 2684354560 | bytes 8388608 | tf_op jit(solution)/shard_map/levels/pallas_call | solution.py:142
  61.4 56.0 %all_to_all.11.back_ref = bf16[128,2,8,1024]{3,2,1,0:T(8,128)(2,1)S(1)} all-to-all(bf16[128,2,8,1024]{3,2,1,0:T(8,128)(2,1)S(1)} %bitcast.7), channel_id=1, replica_groups=mesh['mode'=32,'var'=4] {'var','mode'}, dimensions={0} | all-to-all | bytes 8388608 | tf_op jit(solution)/shard_map/all_to_all | solution.py:194
  117.4 2.1 %place.1 = bf16[2,128,8,1024]{3,2,1,0:T(8,128)(2,1)} custom-call(bf16[128,2,8,1024]{3,2,1,0:T(8,128)(2,1)S(1)} %all_to_all.11.back_ref), custom_call_target="tpu_custom_call" | custom-call | flops 536870912 | bytes 8388608 | tf_op jit(solution)/shard_map/place/pallas_call | solution.py:171
Async XLA Ops:
  17.8 40.7 %copy-start = (bf16[4,512,768]{2,1,0:T(8,128)(2,1)S(1)}, bf16[4,512,768]{2,1,0:T(8,128)(2,1)}, u32[]{:S(2)}) copy-start(bf16[4,512,768]{2,1,0:T(8,128)(2,1)} %get-tuple-element.8.coeff_ref) | copy-start | bytes 9437188

commit v2 on v1

--- a/solution.py
+++ b/solution.py
@@ -35,15 +35,12 @@
 
 
 def smooth_kernel(
-    plane_any, filters_any, weights_any, vertical_any, balance_any,
-    out_ref, coeff_ref,
-    plane_ref, filters_ref, weights_ref, vertical_ref, balance_ref, half_ref, total_ref, sems,
+    plane_any, filters_any, weights_any,
+    out_ref,
+    plane_ref, filters_ref, weights_ref, half_ref, total_ref,
+    sems,
 ):
     count = filters_ref.shape[0]
-    small = [
-        pltpu.make_async_copy(vertical_any, vertical_ref, sems.at[2 * count + 1]),
-        pltpu.make_async_copy(balance_any, balance_ref, sems.at[2 * count + 2]),
-    ]
     plane = pltpu.make_async_copy(plane_any, plane_ref, sems.at[2 * count])
     filters = [
         pltpu.make_async_copy(filters_any.at[k], filters_ref.at[k], sems.at[2 * k])
@@ -53,20 +50,10 @@
         pltpu.make_async_copy(weights_any.at[k], weights_ref.at[k], sems.at[2 * k + 1])
         for k in range(count)
     ]
-    for copy in small:
-        copy.start()
     plane.start()
     for k in range(count):
         filters[k].start()
         weights[k].start()
-
-    for copy in small:
-        copy.wait()
-    modes = vertical_ref.shape[1] * SUB
-    for v in range(vertical_ref.shape[0]):
-        coeff_ref[v, :, :modes] = spread(vertical_ref[v], 0)
-        if v:
-            coeff_ref[v, :, modes:] = spread(balance_ref[v - 1], 1)
 
     plane.wait()
     for k in range(count):
@@ -88,35 +75,33 @@
             out_ref[...] = (total_ref[...] + term).astype(jnp.bfloat16)
 
 
-def smooth(plane, filters, weights, vertical, balance):
+def smooth(plane, filters, weights):
     count, size, _ = filters.shape
-    nvar, modes, levs = vertical.shape
     return pl.pallas_call(
         smooth_kernel,
-        out_shape=[
-            jax.ShapeDtypeStruct((size, size), jnp.bfloat16),
-            jax.ShapeDtypeStruct((nvar, levs * SUB, (modes + levs) * SUB), jnp.bfloat16),
-        ],
-        in_specs=[pl.BlockSpec(memory_space=pl.ANY)] * 5,
+        out_shape=jax.ShapeDtypeStruct((size, size), jnp.bfloat16),
+        in_specs=[pl.BlockSpec(memory_space=pl.ANY)] * 3,
         scratch_shapes=[
             pltpu.VMEM(plane.shape, jnp.bfloat16),
             pltpu.VMEM(filters.shape, jnp.bfloat16),
             pltpu.VMEM(weights.shape, jnp.bfloat16),
-            pltpu.VMEM(vertical.shape, jnp.bfloat16),
-            pltpu.VMEM(balance.shape, jnp.bfloat16),
             pltpu.VMEM((size, size), jnp.bfloat16),
             pltpu.VMEM((size, size), jnp.float32),
-            pltpu.SemaphoreType.DMA((2 * count + 3,)),
+            pltpu.SemaphoreType.DMA((2 * count + 1,)),
         ],
         cost_estimate=cost(4 * count * size**3, 18 * MB),
-        compiler_params=pltpu.CompilerParams(vmem_limit_bytes=67043328),
+        compiler_params=pltpu.CompilerParams(vmem_limit_bytes=52428800),
         name="smooth",
-    )(plane, filters, weights, vertical, balance)
+    )(plane, filters, weights)
 
 
-def level_kernel(blocks_ref, coeff_ref, out_ref):
+def level_kernel(blocks_ref, vertical_ref, balance_ref, out_ref, coeff_ref):
     nvar, modes, _, size = blocks_ref.shape
     deep = modes * SUB
+    for v in range(nvar):
+        coeff_ref[v, :, :deep] = spread(vertical_ref[v], 0)
+        if v:
+            coeff_ref[v, :, deep:] = spread(balance_ref[v - 1], 1)
     for first in range(0, size, WIDE):
         lanes = slice(first, first + WIDE)
         stream = None
@@ -135,19 +120,20 @@
             out_ref[v, :, :, :, lanes] = level.reshape(shape)
 
 
-def mix_levels(blocks, coeff, nmode):
+def mix_levels(blocks, vertical, balance, nmode):
     nvar, modes, _, size = blocks.shape
-    tall = coeff.shape[1]
+    tall = vertical.shape[2] * SUB
     each = tall // SUB // nmode
     return pl.pallas_call(
         level_kernel,
         out_shape=jax.ShapeDtypeStruct((nvar, nmode, each, SUB, size), jnp.bfloat16),
+        scratch_shapes=[pltpu.VMEM((nvar, tall, modes * SUB + tall), jnp.bfloat16)],
         cost_estimate=cost(
             2 * tall * size * (nvar * modes * SUB + (nvar - 1) * tall), 8 * MB
         ),
         compiler_params=vmem(32),
         name="levels",
-    )(blocks, coeff)
+    )(blocks, vertical, balance)
 
 
 def place_kernel(back_ref, out_any, sems):
@@ -186,11 +172,9 @@
     count = nmode * nvar
     each = vertical.shape[1] // nmode
     axes = ("var", "mode")
-    filtered, coeff = smooth(
-        control[0, 0, 0], filters, weights[0], jnp.swapaxes(vertical, 1, 2), balance
-    )
+    filtered = smooth(control[0, 0, 0], filters, weights[0])
     blocks = lax.all_to_all(filtered.reshape(count, SUB, size), axes, 0, 0, tiled=True)
-    result = mix_levels(blocks.reshape(nvar, nmode, SUB, size), coeff, nmode)
+    result = mix_levels(blocks.reshape(nvar, nmode, SUB, size), jnp.swapaxes(vertical, 1, 2), balance, nmode)
     back = lax.all_to_all(result.reshape(count, each, SUB, size), axes, 0, 0, tiled=True)
     return place(back).reshape(1, 1, each, size, size)
 

time: 120 us -> 118 us (0.983)
  Pallas kernels: 22.9 us -> 21.6 us
    pallas_call x1, Pallas kernels: 17.8 us -> 16.4 us  [smooth(): pl.pallas_call(smooth_kernel, out_shape=jax.ShapeDtypeStruct((size, size)...]
where the time goes in v2:
time: 118 us
  blocking collectives  96.5 us (82%)
  Pallas kernels  21.6 us (18%)
    all_to_all x1, blocking collectives, per_device(): lax.all_to_all(result.reshape(count, each, SUB, size), axes, 0, 0, tiled=...  56 us
    all_to_all x1, blocking collectives, per_device(): lax.all_to_all(filtered.reshape(count, SUB, size), axes, 0, 0, tiled=True)  40.5 us
    pallas_call x1, Pallas kernels, smooth(): pl.pallas_call(smooth_kernel, out_shape=jax.ShapeDtypeStruct((size, size)...  16.4 us
    pallas_call x1, Pallas kernels, mix_levels(): pl.pallas_call(level_kernel, out_shape=jax.ShapeDtypeStruct((nvar, nmode,...  3.13 us

profile of v2, /device:TPU:1, one launch (start us, length us, event | category | flops | bytes accessed | tf_op | source)
XLA Modules:
  0.0 118.3 jit_solution(15441702303152282763)
XLA Ops:
  0.0 16.4 %smooth.1 = bf16[1024,1024]{1,0:T(8,128)(2,1)S(1)} custom-call(bf16[1024,1024]{1,0:T(8,128)(2,1)} %bitcast.12, bf16[3,1024,1024]{2,1,0:T(8,128)(2,1)} %filters_any.1, bf16[3,1024,1024]{2,1,0:T(8,128)(2,1)} %bitcast.11), custom_call_target="tpu_custom_call" | custom-call | flops 12884901888 | bytes 18874368 | tf_op jit(solution)/shard_map/smooth/pallas_call | solution.py:80
  16.4 0.0 copy-start
  16.4 0.0 copy-start.1
  16.4 40.5 %all_to_all.10 = bf16[128,8,1024]{2,1,0:T(8,128)(2,1)S(1)} all-to-all(bf16[128,8,1024]{2,1,0:T(8,128)(2,1)S(1)} %bitcast.9), channel_id=1, replica_groups=mesh['mode'=32,'var'=4] {'var','mode'}, dimensions={0} | all-to-all | bytes 4194304 | tf_op jit(solution)/shard_map/all_to_all | solution.py:176
  56.9 0.0 copy-done
  56.9 0.0 copy-done.1
  56.9 3.1 %levels.1 = bf16[4,32,2,8,1024]{4,3,2,1,0:T(8,128)(2,1)S(1)} custom-call(bf16[4,32,8,1024]{3,2,1,0:T(8,128)(2,1)S(1)} %bitcast.8, bf16[4,32,64]{2,1,0:T(8,128)(2,1)S(1)} %bitcast.10, bf16[3,64,64]{2,1,0:T(8,128)(2,1)S(1)} %copy-done), custom_call_target="tpu_custom_call" | custom-call | flops 2684354560 | bytes 8388608 | tf_op jit(solution)/shard_map/levels/pallas_call | solution.py:127
  60.0 56.0 %all_to_all.11.back_ref = bf16[128,2,8,1024]{3,2,1,0:T(8,128)(2,1)S(1)} all-to-all(bf16[128,2,8,1024]{3,2,1,0:T(8,128)(2,1)S(1)} %bitcast.7), channel_id=1, replica_groups=mesh['mode'=32,'var'=4] {'var','mode'}, dimensions={0} | all-to-all | bytes 8388608 | tf_op jit(solution)/shard_map/all_to_all | solution.py:178
  116.0 2.1 %place.1 = bf16[2,128,8,1024]{3,2,1,0:T(8,128)(2,1)} custom-call(bf16[128,2,8,1024]{3,2,1,0:T(8,128)(2,1)S(1)} %all_to_all.11.back_ref), custom_call_target="tpu_custom_call" | custom-call | flops 536870912 | bytes 8388608 | tf_op jit(solution)/shard_map/place/pallas_call | solution.py:157
Async XLA Ops:
  16.4 40.5 %copy-start = (bf16[3,64,64]{2,1,0:T(8,128)(2,1)S(1)}, bf16[3,64,64]{2,1,0:T(8,128)(2,1)}, u32[]{:S(2)}) copy-start(bf16[3,64,64]{2,1,0:T(8,128)(2,1)} %balance_ref.1) | copy-start | bytes 73732
  16.4 40.5 %copy-start.1 = (bf16[4,64,32]{1,2,0:T(8,128)(2,1)S(1)}, bf16[4,64,32]{1,2,0:T(8,128)(2,1)}, u32[]{:S(2)}) copy-start(bf16[4,64,32]{1,2,0:T(8,128)(2,1)} %param.8) | copy-start | bytes 49156

commit v3 on v2

--- a/solution.py
+++ b/solution.py
@@ -42,25 +42,40 @@
 ):
     count = filters_ref.shape[0]
     plane = pltpu.make_async_copy(plane_any, plane_ref, sems.at[2 * count])
+    middle = filters_ref.shape[1] // 2
+    first, second = pl.ds(0, middle), pl.ds(middle, middle)
     filters = [
         pltpu.make_async_copy(filters_any.at[k], filters_ref.at[k], sems.at[2 * k])
-        for k in range(count)
+        for k in range(1, count)
+    ]
+    halves = [
+        pltpu.make_async_copy(filters_any.at[0, at], filters_ref.at[0, at], sems.at[where])
+        for at, where in ((first, 0), (second, 2 * count + 1))
     ]
     weights = [
         pltpu.make_async_copy(weights_any.at[k], weights_ref.at[k], sems.at[2 * k + 1])
         for k in range(count)
     ]
     plane.start()
-    for k in range(count):
-        filters[k].start()
+    for copy in halves + weights[:1]:
+        copy.start()
+    for k in range(1, count):
+        filters[k - 1].start()
         weights[k].start()
 
     plane.wait()
     for k in range(count):
-        filters[k].wait()
-        half_ref[...] = jnp.dot(
-            filters_ref[k], plane_ref[...], preferred_element_type=jnp.float32
-        ).astype(jnp.bfloat16)
+        if k:
+            filters[k - 1].wait()
+            half_ref[...] = jnp.dot(
+                filters_ref[k], plane_ref[...], preferred_element_type=jnp.float32
+            ).astype(jnp.bfloat16)
+        else:
+            for copy, at in zip(halves, (first, second)):
+                copy.wait()
+                half_ref[at, :] = jnp.dot(
+                    filters_ref[0, at, :], plane_ref[...], preferred_element_type=jnp.float32
+                ).astype(jnp.bfloat16)
         weights[k].wait()
         full = lax.dot_general(
             half_ref[...], filters_ref[k], (((1,), (1,)), ((), ())),
@@ -87,7 +102,7 @@
             pltpu.VMEM(weights.shape, jnp.bfloat16),
             pltpu.VMEM((size, size), jnp.bfloat16),
             pltpu.VMEM((size, size), jnp.float32),
-            pltpu.SemaphoreType.DMA((2 * count + 1,)),
+            pltpu.SemaphoreType.DMA((2 * count + 2,)),
         ],
         cost_estimate=cost(4 * count * size**3, 18 * MB),
         compiler_params=pltpu.CompilerParams(vmem_limit_bytes=52428800),

time: 118 us -> 118 us (level)
  no operation moved by 1% of the time
where the time goes in v3:
time: 118 us
  blocking collectives  96.5 us (82%)
  Pallas kernels  21.5 us (18%)
    all_to_all x1, blocking collectives, per_device(): lax.all_to_all(result.reshape(count, each, SUB, size), axes, 0, 0, tiled=...  56 us
    all_to_all x1, blocking collectives, per_device(): lax.all_to_all(filtered.reshape(count, SUB, size), axes, 0, 0, tiled=True)  40.5 us
    pallas_call x1, Pallas kernels, smooth(): pl.pallas_call(smooth_kernel, out_shape=jax.ShapeDtypeStruct((size, size)...  16.2 us
    pallas_call x1, Pallas kernels, mix_levels(): pl.pallas_call(level_kernel, out_shape=jax.ShapeDtypeStruct((nvar, nmode,...  3.13 us

profile of v3, /device:TPU:1, one launch (start us, length us, event | category | flops | bytes accessed | tf_op | source)
XLA Modules:
  0.0 118.1 jit_solution(6910975861178848565)
XLA Ops:
  0.0 16.2 %smooth.1 = bf16[1024,1024]{1,0:T(8,128)(2,1)S(1)} custom-call(bf16[1024,1024]{1,0:T(8,128)(2,1)} %bitcast.12, bf16[3,1024,1024]{2,1,0:T(8,128)(2,1)} %filters_any.1, bf16[3,1024,1024]{2,1,0:T(8,128)(2,1)} %bitcast.11), custom_call_target="tpu_custom_call" | custom-call | flops 12884901888 | bytes 18874368 | tf_op jit(solution)/shard_map/smooth/pallas_call | solution.py:95
  16.2 0.0 copy-start
  16.2 0.0 copy-start.1
  16.2 40.5 %all_to_all.10 = bf16[128,8,1024]{2,1,0:T(8,128)(2,1)S(1)} all-to-all(bf16[128,8,1024]{2,1,0:T(8,128)(2,1)S(1)} %bitcast.9), channel_id=1, replica_groups=mesh['mode'=32,'var'=4] {'var','mode'}, dimensions={0} | all-to-all | bytes 4194304 | tf_op jit(solution)/shard_map/all_to_all | solution.py:191
  56.7 0.0 copy-done
  56.7 0.0 copy-done.1
  56.7 3.1 %levels.1 = bf16[4,32,2,8,1024]{4,3,2,1,0:T(8,128)(2,1)S(1)} custom-call(bf16[4,32,8,1024]{3,2,1,0:T(8,128)(2,1)S(1)} %bitcast.8, bf16[4,32,64]{2,1,0:T(8,128)(2,1)S(1)} %bitcast.10, bf16[3,64,64]{2,1,0:T(8,128)(2,1)S(1)} %copy-done), custom_call_target="tpu_custom_call" | custom-call | flops 2684354560 | bytes 8388608 | tf_op jit(solution)/shard_map/levels/pallas_call | solution.py:142
  59.8 56.0 %all_to_all.11.back_ref = bf16[128,2,8,1024]{3,2,1,0:T(8,128)(2,1)S(1)} all-to-all(bf16[128,2,8,1024]{3,2,1,0:T(8,128)(2,1)S(1)} %bitcast.7), channel_id=1, replica_groups=mesh['mode'=32,'var'=4] {'var','mode'}, dimensions={0} | all-to-all | bytes 8388608 | tf_op jit(solution)/shard_map/all_to_all | solution.py:193
  115.8 2.1 %place.1 = bf16[2,128,8,1024]{3,2,1,0:T(8,128)(2,1)} custom-call(bf16[128,2,8,1024]{3,2,1,0:T(8,128)(2,1)S(1)} %all_to_all.11.back_ref), custom_call_target="tpu_custom_call" | custom-call | flops 536870912 | bytes 8388608 | tf_op jit(solution)/shard_map/place/pallas_call | solution.py:172
Async XLA Ops:
  16.2 40.5 %copy-start = (bf16[3,64,64]{2,1,0:T(8,128)(2,1)S(1)}, bf16[3,64,64]{2,1,0:T(8,128)(2,1)}, u32[]{:S(2)}) copy-start(bf16[3,64,64]{2,1,0:T(8,128)(2,1)} %balance_ref.1) | copy-start | bytes 73732
  16.2 40.5 %copy-start.1 = (bf16[4,64,32]{1,2,0:T(8,128)(2,1)S(1)}, bf16[4,64,32]{1,2,0:T(8,128)(2,1)}, u32[]{:S(2)}) copy-start(bf16[4,64,32]{1,2,0:T(8,128)(2,1)} %param.8) | copy-start | bytes 49156
